TPU v7x, 32 devices: a whole 2x2x4 slice. The times are simulated.
32 devices in a mesh: space: 16 (over z, y, x), grp: 2 (over core).
Axes of the slice: x: 2, y: 2, z: 4, core: 2. Of those that a mesh axis runs over, the one named last changes fastest.
Arguments:
- echoes: bfloat16 [160, 300, 2048], P(('space', 'grp'))
- frame_count: int32 [160], replicated, may hold values from 0 to 300, as said below
- clutter_rank: int32 [160], replicated, may hold values from 1 to 24
- noise_rank: int32 [160], replicated, may hold values from 48 to 96
- start_basis: float32 [300, 96], replicated, may hold values from -6 to 6
Outputs:
- volume: float32 [300, 163840], P(None, ('space', 'grp'))
- power: float32 [163840], P(('space', 'grp'))
Inputs may be any that keep to these rules, and one draw needn't show every extreme that they name: `frame_count`: within each holder's 5 consecutive slots the slots with frames come first and the others have 0 frames; every holder has 1 to 5 slots with frames, some holder has all 5; two holders with the same grp index whose space indices lie half the space axis apart have at most 6 slots with frames together; a slot with frames has 150 or more.
All inputs are finite; a program needn't handle non-finite values.
Results may differ from a plain program's by a relative error of at most 0.0056.
Values may be sent and summed in bfloat16 or wider, within the bound.
No kernel may reach another device: no remote copies, remote signals or barrier semaphores. Data moves between devices by JAX's collectives and lax.ppermute only.
A program may use at most 128 MiB of HBM per device.

v0:
```python
import jax
import jax.numpy as jnp
from jax import lax
from jax.sharding import PartitionSpec as P

ITERS = 4


def passed_along(value, axis, steps):
    count = lax.axis_size(axis)
    initial, last = (max(0, -steps), min(count, count - steps))
    return lax.ppermute(value, axis, [(source, source + steps) for source in range(initial, last)])


def filter_block(echo_block, frame_total, clutter_cut, noise_cut, initial):
    frames = jnp.arange(echo_block.shape[0], dtype=jnp.int32)
    frame_mask = (frames < frame_total).astype(jnp.bfloat16)
    padding_diag = (frames >= frame_total).astype(jnp.float32)
    masked = echo_block * frame_mask[:, None]
    gram_matrix = jnp.dot(masked, masked.T, preferred_element_type=jnp.float32) + jnp.diag(
        padding_diag
    )
    subspace = initial
    for iteration in range(ITERS):
        product = jnp.dot(gram_matrix, subspace, precision=lax.Precision.HIGHEST)
        inner_gram = jnp.dot(product.T, product, precision=lax.Precision.HIGHEST)
        factor = jnp.linalg.cholesky(inner_gram)
        subspace = jax.scipy.linalg.solve_triangular(factor, product.T, lower=True).T
    basis = subspace.astype(jnp.bfloat16)
    coefficients = jnp.dot(basis.T, masked, preferred_element_type=jnp.float32)
    columns = jnp.arange(basis.shape[1], dtype=jnp.int32)
    band_mask = ((columns >= clutter_cut) & (columns < noise_cut)).astype(jnp.float32)
    coefficients = (coefficients * band_mask[:, None]).astype(jnp.bfloat16)
    return jnp.dot(basis, coefficients, preferred_element_type=jnp.float32).astype(jnp.bfloat16)


def block_ints(device, hold, frame_count, clutter_rank, noise_rank):
    first_block = device * hold
    return tuple(
        (
            lax.dynamic_slice_in_dim(source, first_block, hold)
            for source in (frame_count, clutter_rank, noise_rank)
        )
    )


def shards(echoes, frame_count, clutter_rank, noise_rank, start_basis):
    space_count = lax.axis_size("space")
    pair_count = lax.axis_size("grp")
    hold = echoes.shape[0]
    space_index = lax.axis_index("space")
    grp_index = lax.axis_index("grp")
    device = space_index * pair_count + grp_index
    frames_home, clutter_home, noise_home = block_ints(
        device, hold, frame_count, clutter_rank, noise_rank
    )
    runner = jax.vmap(filter_block, in_axes=(0, 0, 0, 0, None))
    cleaned_home = runner(echoes, frames_home, clutter_home, noise_home, start_basis)
    width = cleaned_home.shape[2]
    half_width = width // 2
    window = jnp.sin(jnp.pi * (jnp.arange(width, dtype=jnp.float32) + 0.5) / width) ** 2
    weighted = cleaned_home.astype(jnp.float32) * window
    border_raw = passed_along(cleaned_home[0, :, :half_width], ("space", "grp"), -1)
    border = border_raw.astype(jnp.float32) * window[:half_width]
    following = jnp.concatenate([weighted[1:, :, :half_width], border[None]], axis=0)
    regions = weighted[:, :, half_width:] + following
    frames_total = regions.shape[1]
    volume = jnp.transpose(regions, (1, 0, 2)).reshape(frames_total, -1)
    strength = jnp.sum(volume * volume, axis=0) / frames_total
    total = lax.psum(jnp.sum(strength), ("space", "grp"))
    mean_level = total / (strength.shape[0] * space_count * pair_count)
    power = strength / (mean_level + 1e-06)
    return (volume, power)


def solution(mesh):
    return jax.shard_map(
        shards,
        mesh=mesh,
        in_specs=(P(("space", "grp"), None, None), P(), P(), P(), P()),
        out_specs=(P(None, ("space", "grp")), P(("space", "grp"))),
        check_vma=False,
    )
```

profile of v0, /device:TPU:0, one launch (start us, length us, event | category | flops | bytes accessed | tf_op | source)
XLA Modules:
  0.0 459.2 jit_solution(15295016572012153055)
XLA Ops:
  3.1 8.1 %select_add_fusion = f32[5,300,300]{2,1,0:T(8,128)S(1)} fusion(bf16[5,300,2048]{2,1,0:T(8,128)(2,1)} %param.8, bf16[5,300]{1,0:T(8,128)(2,1)S(1)} %get-tuple-element.11, f32[5,300]{1,0:T(8,128)S(1)} %get-tuple-element.10, pred[300,300]{1,0:T(8,128)(4,1)S(1)} %iota_compare_fusion), kind=kOutput, calls=%fused_computation.12 | convolution fusion | flops 1847172096 | bytes 8043000 | tf_op jit(solution)/shard_map/vmap()/dot_general | solution.py:20
  11.2 2.7 fusion.29
  13.9 1.0 fusion.38
  15.8 1.7 fusion.28
  17.4 44.9 %custom-call.12 = f32[5,96,96]{2,1,0:T(8,128)S(1)} custom-call(f32[5,96,96]{2,1,0:T(8,128)} %fusion.28), custom_call_target="Cholesky" | custom-call | tf_op jit(solution)/shard_map/vmap(jit(cholesky))/cholesky | solution.py:27
  63.3 37.6 %custom-call.13 = f32[5,1,96,96]{2,3,1,0:T(8,128)S(1)} custom-call(f32[5,1,96,96]{3,2,1,0:T(8,128)} %select_bitcast_fusion.3), custom_call_target="InvertDiagBlocksLowerTriangular" | custom-call | tf_op jit(solution)/shard_map/vmap(jit(_solve_triangular))/triangular_solve | solution.py:28
  100.9 0.8 fusion.19
  101.8 2.7 fusion.39
  104.5 1.0 fusion.40
  106.3 1.7 fusion.26
  108.0 44.7 %custom-call.14 = f32[5,96,96]{2,1,0:T(8,128)S(1)} custom-call(f32[5,96,96]{2,1,0:T(8,128)} %fusion.26), custom_call_target="Cholesky" | custom-call | tf_op jit(solution)/shard_map/vmap(jit(cholesky))/cholesky | solution.py:27
  153.7 37.9 %custom-call.15 = f32[5,1,96,96]{2,3,1,0:T(8,128)S(1)} custom-call(f32[5,1,96,96]{3,2,1,0:T(8,128)} %select_bitcast_fusion.2), custom_call_target="InvertDiagBlocksLowerTriangular" | custom-call | tf_op jit(solution)/shard_map/vmap(jit(_solve_triangular))/triangular_solve | solution.py:28
  191.5 0.8 fusion.17
  192.4 2.7 fusion.41
  195.1 1.0 fusion.42
  196.9 1.7 fusion.24
  198.6 44.7 %custom-call.16 = f32[5,96,96]{2,1,0:T(8,128)S(1)} custom-call(f32[5,96,96]{2,1,0:T(8,128)} %fusion.24), custom_call_target="Cholesky" | custom-call | tf_op jit(solution)/shard_map/vmap(jit(cholesky))/cholesky | solution.py:27
  244.3 37.9 %custom-call.17 = f32[5,1,96,96]{2,3,1,0:T(8,128)S(1)} custom-call(f32[5,1,96,96]{3,2,1,0:T(8,128)} %select_bitcast_fusion.1), custom_call_target="InvertDiagBlocksLowerTriangular" | custom-call | tf_op jit(solution)/shard_map/vmap(jit(_solve_triangular))/triangular_solve | solution.py:28
  282.2 0.8 fusion.15
  283.0 2.7 fusion.43
  285.7 1.0 fusion.44
  286.9 44.0 %custom-call.18 = f32[5,96,96]{2,1,0:T(8,128)S(1)} custom-call(f32[5,96,96]{2,1,0:T(8,128)S(1)} %fusion.22), custom_call_target="Cholesky" | custom-call | tf_op jit(solution)/shard_map/vmap(jit(cholesky))/cholesky | solution.py:27
  331.1 36.9 %custom-call.19 = f32[5,1,96,96]{2,3,1,0:T(8,128)S(1)} custom-call(f32[5,1,96,96]{3,2,1,0:T(8,128)S(1)} %select_bitcast_fusion), custom_call_target="InvertDiagBlocksLowerTriangular" | custom-call | tf_op jit(solution)/shard_map/vmap(jit(_solve_triangular))/triangular_solve | solution.py:28
  368.0 0.8 convolution_convert_fusion.1
  368.9 12.7 %convert_multiply_fusion = (f32[5,300,2048]{2,1,0:T(8,128)}, bf16[5,300,2048]{2,1,0:T(8,128)(2,1)}) fusion(f32[2048]{0:T(1024)S(1)} %sine_multiply_fusion, bf16[5,96,300]{2,1,0:T(8,128)(2,1)S(1)} %convolution_convert_fusion.1, bf16[5,300,2048]{2,1,0:T(8,128)(2,1)} %param.8, bf16[5,300]{1,0:T(8,128)(2,1)S(1)} %get-tuple-element.11, f32[5,96]{1,0:T(8,128)S(1)} %fusion.34), kind=kOutput, calls=%fused_computation | convolution fusion | flops 1193902080 | bytes 24877112 | tf_op jit(solution)/shard_map/vmap()/dot_general | solution.py:34
  381.6 1.3 slice_bitcast_fusion
  382.9 1.8 collective-permute-start
  384.7 3.4 slice.25
  388.3 3.5 multiply_reduce_fusion
  392.4 48.3 %psum.7 = f32[]{:T(128)} all-reduce(f32[]{:T(128)} %multiply_reduce_fusion.1), channel_id=1, replica_groups=mesh['space'=16,'grp'=2] {'space','grp'}, use_global_device_ids=true, to_apply=%region_4.7 | all-reduce | flops 1 | bytes 8 | tf_op jit(solution)/shard_map/psum | solution.py:70
  442.0 8.3 %copy.27 = f32[300,5,1024]{0,2,1:T(8,128)} copy(f32[300,5,1024]{2,0,1:T(8,128)} %get-tuple-element.9) | data formatting | bytes 12288000 | tf_op jit(solution)/shard_map/transpose | solution.py:68
  450.3 8.4 %copy.28 = f32[300,5120]{1,0:T(8,128)} copy(f32[300,5120]{0,1:T(8,128)} %bitcast.76) | data formatting | bytes 12288000
  (36 shorter events, 9.7 us)
Async XLA Ops:
  0.6 10.6 %copy-start = (f32[300,96]{0,1:T(8,128)S(1)}, f32[300,96]{0,1:T(8,128)}, u32[]{:S(2)}) copy-start(f32[300,96]{0,1:T(8,128)} %param.12) | copy-start | bytes 345604
  381.6 6.7 %copy-start.1 = (f32[5,300,2048]{2,1,0:T(8,128)S(1)}, f32[5,300,2048]{2,1,0:T(8,128)}, u32[]{:S(2)}) copy-start(f32[5,300,2048]{2,1,0:T(8,128)} %get-tuple-element.12) | copy-start | bytes 36864004
  382.9 5.3 %collective-permute-start = (bf16[300,1024]{1,0:T(8,128)(2,1)S(1)}, bf16[300,1024]{1,0:T(8,128)(2,1)S(1)}, u32[]{:S(2)}, u32[]{:S(2)}) collective-permute-start(bf16[300,1024]{1,0:T(8,128)(2,1)S(1)} %slice_bitcast_fusion), channel_id=1, source_target_pairs={{1,0},{2,1},{3,2},{4,3},{5,4},{6,5},{7,6},{8,7},{9,8},{10,9},{11,1... | collective-permute-start | bytes 1843208 | tf_op jit(solution)/shard_map/ppermute | solution.py:12
where the time goes:
time: 465 us; the launch traced here: 459 us
  other arithmetic  341 us (73%)
  blocking collectives  48.3 us (10%)
  matrix products  38.8 us (8%)
  local copies, waits for them, and re-layouts  26.9 us (6%)
    another operation x13, other arithmetic, filter_block(): factor = jnp.linalg.cholesky(inner_gram)  179 us
    another operation x9, other arithmetic, filter_block(): jax.scipy.linalg.solve_triangular(factor, product.T, lower=True)  153 us
    psum x1, blocking collectives, shards(): total = lax.psum(jnp.sum(strength), ('space', 'grp'))  48.3 us
    dot_general x1, matrix products, filter_block(): jnp.dot(basis, coefficients, preferred_element_type=jnp.float32)  12.7 us
    dot_general x4, matrix products, filter_block(): product = jnp.dot(gram_matrix, subspace, precision=lax.Precision.HIGHEST)  10.7 us
  transfers between devices with their start and end apart: 1, of which 0 were waited for; matrix products, arithmetic and copies ran while one was open for 1% of the time, Pallas kernels for 0%

commit v1 on v0

v1 whole, which is shorter than its diff:
```python
import functools

import jax
import jax.numpy as jnp
from jax import lax
from jax.experimental import pallas as pl
from jax.experimental.pallas import tpu as pltpu
from jax.sharding import PartitionSpec as P

ITERS = 4
LANES = 128
SLOTS = 8
PANEL = 8
SUPER = 32
HIGHEST = lax.Precision.HIGHEST


def round_up(value, unit):
    return -(-value // unit) * unit


def device_index():
    return lax.axis_index("space") * lax.axis_size("grp") + lax.axis_index("grp")


def inverse_factors(rows_ref, scaled_ref, out_ref, order, hold, out_stride):
    lane = lax.broadcasted_iota(jnp.int32, (SLOTS, LANES), 1)

    def spread(value, index):
        return jnp.broadcast_to(value[:, index : index + 1], (SLOTS, LANES))

    for start in range(0, order, SUPER):
        stop = min(start + SUPER, order)
        for base in range(start, stop, PANEL):
            panel = (lane >= base) & (lane < base + PANEL)
            rows = [rows_ref[(base + r) * SLOTS : (base + r + 1) * SLOTS, :] for r in range(PANEL)]
            block = {
                (r, c): spread(rows[r], base + c) for r in range(PANEL) for c in range(r, PANEL)
            }
            rows = [
                jnp.where(panel, jnp.where(lane == base + r, 1.0, 0.0), rows[r])
                for r in range(PANEL)
            ]
            scaled = []
            for j in range(PANEL):
                inverse = 1.0 / block[j, j]
                scaled.append(rows[j] * inverse)
                for r in range(j + 1, PANEL):
                    factor = block[j, r] * inverse
                    rows[r] = rows[r] - factor * rows[j]
                    for c in range(r, PANEL):
                        block[r, c] = block[r, c] - factor * block[j, c]
            for j in range(PANEL):
                out_ref[pl.ds(base + j, SLOTS, stride=out_stride), :] = jnp.where(
                    lane < base + PANEL, rows[j] * lax.rsqrt(block[j, j]), 0.0
                )
            if stop < order:
                later = (lane >= base + PANEL) & (lane < stop)
                for j in range(PANEL):
                    rows_ref[(base + j) * SLOTS : (base + j + 1) * SLOTS, :] = jnp.where(
                        later, 0.0, rows[j]
                    )
                    at = base - start + j
                    scaled_ref[at * SLOTS : (at + 1) * SLOTS, :] = scaled[j]
            for r in range(base + PANEL, stop):
                total = jnp.where(panel, 0.0, rows_ref[r * SLOTS : (r + 1) * SLOTS, :])
                for j in range(PANEL):
                    total = total - spread(scaled[j], r) * rows[j]
                rows_ref[r * SLOTS : (r + 1) * SLOTS, :] = total
        if stop < order:
            rest = order - stop
            wide_lane = lax.broadcasted_iota(jnp.int32, (rest, LANES), 1)
            done = (wide_lane >= start) & (wide_lane < stop)
            for b in range(hold):
                upper = rows_ref[pl.ds(start * SLOTS + b, stop - start, stride=SLOTS), :]
                lower = scaled_ref[pl.ds(b, stop - start, stride=SLOTS), :]
                update = jnp.dot(
                    lower.T[stop:order, :],
                    upper,
                    precision=HIGHEST,
                    preferred_element_type=jnp.float32,
                )
                where = pl.ds(stop * SLOTS + b, rest, stride=SLOTS)
                rows_ref[where, :] = jnp.where(done, 0.0, rows_ref[where, :]) - update


def basis_kernel(
    frame_ref,
    clutter_ref,
    noise_ref,
    start_ref,
    echo_hbm,
    basis_ref,
    border_ref,
    echo_ref,
    sems,
    gram_ref,
    sub_ref,
    prod_ref,
    rows_ref,
    scaled_ref,
    factor_ref,
):
    hold, frames, width = echo_hbm.shape
    order = start_ref.shape[1]
    tall = basis_ref.shape[1]
    deep = sub_ref.shape[1]
    half = width // 2
    first = device_index() * hold
    copies = [
        pltpu.make_async_copy(echo_hbm.at[b], echo_ref.at[b], sems.at[b]) for b in range(hold)
    ]
    for copy in copies:
        copy.start()
    sub_ref[...] = jnp.zeros_like(sub_ref)
    prod_ref[...] = jnp.zeros_like(prod_ref)
    rows_ref[...] = jnp.zeros_like(rows_ref)
    factor_ref[...] = jnp.zeros_like(factor_ref)
    gram_ref[...] = jnp.zeros_like(gram_ref)
    for b in range(hold):
        sub_ref[b, :frames, :order] = start_ref[...]
    row_at = lax.broadcasted_iota(jnp.int32, (frames, frames), 0)
    column_at = lax.broadcasted_iota(jnp.int32, (frames, frames), 1)
    for b in range(hold):
        copies[b].wait()
        echo = echo_ref[b]
        valid = frame_ref[first + b]
        gram = lax.dot_general(
            echo, echo, (((1,), (1,)), ((), ())), preferred_element_type=jnp.float32
        )
        padding = jnp.where((row_at == column_at) & (row_at >= valid), 1.0, 0.0)
        gram_ref[b, :frames, :frames] = jnp.where(
            (row_at < valid) & (column_at < valid), gram, padding
        )

    def iteration(_, carry):
        for b in range(hold):
            product = jnp.dot(
                gram_ref[b], sub_ref[b], precision=HIGHEST, preferred_element_type=jnp.float32
            )
            prod_ref[b, :tall, :] = product
            whole = prod_ref[b]
            inner = lax.dot_general(
                whole,
                whole,
                (((0,), (0,)), ((), ())),
                precision=HIGHEST,
                preferred_element_type=jnp.float32,
            )
            rows_ref[pl.ds(b, order, stride=SLOTS), :] = inner[:order, :]
        inverse_factors(rows_ref, scaled_ref, factor_ref, order, hold, LANES)
        for b in range(hold):
            sub_ref[b, :tall, :] = lax.dot_general(
                prod_ref[b, :tall, :],
                factor_ref[b * LANES : (b + 1) * LANES, :],
                (((1,), (1,)), ((), ())),
                precision=HIGHEST,
                preferred_element_type=jnp.float32,
            )
        return carry

    lax.fori_loop(0, ITERS, iteration, 0)
    for b in range(hold):
        basis_ref[b] = sub_ref[b, :tall, :].astype(jnp.bfloat16)
    basis = sub_ref[0].T.astype(jnp.bfloat16)[:order, :]
    frame_at = lax.broadcasted_iota(jnp.int32, (order, frames), 1)
    kept = jnp.where(frame_at < frame_ref[first], basis[:, :frames], jnp.zeros((), jnp.bfloat16))
    low = jnp.dot(kept, echo_ref[0, :, :half], preferred_element_type=jnp.float32)
    column = lax.broadcasted_iota(jnp.int32, (order, 1), 0)
    band = (column >= clutter_ref[first]) & (column < noise_ref[first])
    border_ref[:, :half] = jnp.where(band, low, 0.0).astype(jnp.bfloat16)
    border_ref[:, half:] = basis


def find_bases(echoes, frame_count, clutter_rank, noise_rank, start_basis):
    hold, frames, width = echoes.shape
    order = start_basis.shape[1]
    tall = round_up(frames, 16)
    deep = round_up(frames, LANES)
    smem = pl.BlockSpec(memory_space=pltpu.SMEM)
    vmem = pl.BlockSpec(memory_space=pltpu.VMEM)
    return pl.pallas_call(
        basis_kernel,
        out_shape=(
            jax.ShapeDtypeStruct((hold, tall, LANES), jnp.bfloat16),
            jax.ShapeDtypeStruct((order, width // 2 + deep), jnp.bfloat16),
        ),
        in_specs=[smem, smem, smem, vmem, pl.BlockSpec(memory_space=pl.ANY)],
        out_specs=(vmem, vmem),
        scratch_shapes=[
            pltpu.VMEM((hold, frames, width), jnp.bfloat16),
            pltpu.SemaphoreType.DMA((hold,)),
            pltpu.VMEM((hold, tall, deep), jnp.float32),
            pltpu.VMEM((hold, deep, LANES), jnp.float32),
            pltpu.VMEM((hold, deep, LANES), jnp.float32),
            pltpu.VMEM((order * SLOTS, LANES), jnp.float32),
            pltpu.VMEM((SUPER * SLOTS, LANES), jnp.float32),
            pltpu.VMEM((SLOTS * LANES, LANES), jnp.float32),
        ],
        name="find_bases",
    )(frame_count, clutter_rank, noise_rank, start_basis, echoes)


def projected(basis, echo, valid, low, high, order):
    frames = echo.shape[0]
    frame_at = lax.broadcasted_iota(jnp.int32, (order, frames), 1)
    flipped = basis.astype(jnp.float32).T.astype(jnp.bfloat16)[:order, :frames]
    kept = jnp.where(frame_at < valid, flipped, jnp.zeros((), jnp.bfloat16))
    coefficients = jnp.dot(kept, echo, preferred_element_type=jnp.float32)
    column = lax.broadcasted_iota(jnp.int32, (order, 1), 0)
    band = (column >= low) & (column < high)
    coefficients = jnp.where(band, coefficients, 0.0).astype(jnp.bfloat16)
    cleaned = jnp.dot(basis[:frames, :order], coefficients, preferred_element_type=jnp.float32)
    return cleaned.astype(jnp.bfloat16).astype(jnp.float32)


def region_kernel(
    frame_ref,
    clutter_ref,
    noise_ref,
    window_ref,
    upper_ref,
    lower_ref,
    basis_ref,
    volume_ref,
    strength_ref,
    order,
):
    hold = basis_ref.shape[0]
    frames, half = volume_ref.shape
    region = pl.program_id(0)
    at = device_index() * hold + region
    own = projected(
        basis_ref[region, :, :], upper_ref[0], frame_ref[at], clutter_ref[at], noise_ref[at], order
    )
    total = own * window_ref[:, half:]
    volume_ref[...] = total

    @pl.when(region < hold - 1)
    def _():
        next_one = projected(
            basis_ref[region + 1, :, :],
            lower_ref[0],
            frame_ref[at + 1],
            clutter_ref[at + 1],
            noise_ref[at + 1],
            order,
        )
        both = volume_ref[...] + next_one * window_ref[:, :half]
        volume_ref[...] = both
        strength_ref[...] = jnp.sum(both * both, axis=0, keepdims=True) / frames


def compound(echoes, basis, window, frame_count, clutter_rank, noise_rank, order):
    hold, frames, width = echoes.shape
    half = width // 2
    smem = pl.BlockSpec(memory_space=pltpu.SMEM)
    return pl.pallas_call(
        functools.partial(region_kernel, order=order),
        grid=(hold,),
        out_shape=(
            jax.ShapeDtypeStruct((frames, hold * half), jnp.float32),
            jax.ShapeDtypeStruct((1, hold * half), jnp.float32),
        ),
        in_specs=[
            smem,
            smem,
            smem,
            pl.BlockSpec((1, width), lambda r: (0, 0)),
            pl.BlockSpec((1, frames, half), lambda r: (r, 0, 1)),
            pl.BlockSpec((1, frames, half), lambda r: (jnp.minimum(r + 1, hold - 1), 0, 0)),
            pl.BlockSpec(basis.shape, lambda r: (0, 0, 0)),
        ],
        out_specs=(
            pl.BlockSpec((frames, half), lambda r: (0, r)),
            pl.BlockSpec((1, half), lambda r: (0, r)),
        ),
        cost_estimate=pl.CostEstimate(
            flops=hold * 4 * frames * order * width,
            bytes_accessed=hold * frames * width * 4,
            transcendentals=0,
        ),
        name="compound",
    )(frame_count, clutter_rank, noise_rank, window, echoes, echoes, basis)


def border_kernel(window_ref, border_ref, region_ref, strength_ref, volume_ref, all_ref, sums_ref):
    frames, half = region_ref.shape
    order = border_ref.shape[0]
    lengths = strength_ref.shape[1]
    flipped = border_ref[:, half:].astype(jnp.float32).T.astype(jnp.bfloat16)[:frames, :]
    cleaned = jnp.dot(flipped, border_ref[:, :half], preferred_element_type=jnp.float32)
    cleaned = cleaned.astype(jnp.bfloat16).astype(jnp.float32)
    both = region_ref[...] + cleaned * window_ref[:, :half]
    volume_ref[...] = both
    last = jnp.sum(both * both, axis=0, keepdims=True) / frames
    all_ref[:, : lengths - half] = strength_ref[:, : lengths - half]
    all_ref[:, lengths - half :] = last
    total = jnp.sum(strength_ref[:, : lengths - half]) + jnp.sum(last)
    sums_ref[...] = jnp.full(sums_ref.shape, total, jnp.float32)


def close_border(window, border, volume, strength, hold, devices):
    frames, voxels = volume.shape
    half = voxels // hold
    return pl.pallas_call(
        border_kernel,
        grid=(1,),
        out_shape=(
            jax.ShapeDtypeStruct(volume.shape, jnp.float32),
            jax.ShapeDtypeStruct(strength.shape, jnp.float32),
            jax.ShapeDtypeStruct((devices, LANES), jnp.float32),
        ),
        in_specs=[
            pl.BlockSpec(window.shape, lambda i: (0, 0)),
            pl.BlockSpec(border.shape, lambda i: (0, 0)),
            pl.BlockSpec((frames, half), lambda i: (0, hold - 1)),
            pl.BlockSpec(strength.shape, lambda i: (0, 0)),
        ],
        out_specs=(
            pl.BlockSpec((frames, half), lambda i: (0, hold - 1)),
            pl.BlockSpec(strength.shape, lambda i: (0, 0)),
            pl.BlockSpec((devices, LANES), lambda i: (0, 0)),
        ),
        input_output_aliases={2: 0},
        name="close_border",
    )(window, border, volume, strength)


def power_kernel(strength_ref, sums_ref, power_ref):
    voxels = strength_ref.shape[1] * sums_ref.shape[0]
    total = jnp.sum(sums_ref[:, :1])
    power_ref[...] = (strength_ref[...] / (total / voxels + 1e-06))[0]


def relative_power(strength, sums):
    vmem = pl.BlockSpec(memory_space=pltpu.VMEM)
    return pl.pallas_call(
        power_kernel,
        out_shape=jax.ShapeDtypeStruct((strength.shape[1],), jnp.float32),
        in_specs=[vmem, vmem],
        out_specs=vmem,
        name="relative_power",
    )(strength, sums)


def shards(echoes, frame_count, clutter_rank, noise_rank, start_basis):
    axes = ("space", "grp")
    devices = lax.axis_size("space") * lax.axis_size("grp")
    hold, frames, width = echoes.shape
    order = start_basis.shape[1]
    window = jnp.sin(jnp.pi * (jnp.arange(width, dtype=jnp.float32) + 0.5) / width) ** 2
    window = window[None, :]
    basis, border = find_bases(echoes, frame_count, clutter_rank, noise_rank, start_basis)
    border = lax.ppermute(border, axes, [(source, source - 1) for source in range(1, devices)])
    volume, strength = compound(
        echoes, basis, window, frame_count, clutter_rank, noise_rank, order
    )
    volume, strength, sums = close_border(window, border, volume, strength, hold, devices)
    sums = lax.all_to_all(sums, axes, 0, 0, tiled=True)
    return volume, relative_power(strength, sums)


def solution(mesh):
    return jax.shard_map(
        shards,
        mesh=mesh,
        in_specs=(P(("space", "grp"), None, None), P(), P(), P(), P()),
        out_specs=(P(None, ("space", "grp")), P(("space", "grp"))),
        check_vma=False,
    )
```

time: 465 us -> 77.3 us (0.17); the launches traced: 459 us -> 76.9 us
  other arithmetic: 341 us -> 0.83 us
  Pallas kernels: 0 us -> 56.3 us
  matrix products: 38.8 us -> 0 us
  blocking collectives: 48.3 us -> 15.4 us
  local copies, waits for them, and re-layouts: 26.9 us -> 2.39 us
    another operation x22 -> x0, other arithmetic: 332 us -> none  [the longest x13 179 us: filter_block(): factor = jnp.linalg.cholesky(inner_gram)]
    pallas_call x0 -> x4, Pallas kernels: none -> 56.3 us  [the longest x1 43.3 us: find_bases(): pl.pallas_call(basis_kernel, out_shape=(jax.ShapeDtypeStruct((hold, tall,...]
    psum x1 -> x0, blocking collectives: 48.3 us -> none  [shards(): total = lax.psum(jnp.sum(strength), ('space', 'grp'))]
    dot_general x10 -> x0, matrix products: 35.5 us -> none  [the longest x1 12.7 us: filter_block(): jnp.dot(basis, coefficients, preferred_element_type=jnp.float32)]
    all_to_all x0 -> x1, blocking collectives: none -> 15.4 us  [shards(): sums = lax.all_to_all(sums, axes, 0, 0, tiled=True)]
    transpose x1 -> x0, local copies, waits for them, and re-layouts: 8.29 us -> none  [shards(): volume = jnp.transpose(regions, (1, 0, 2)).reshape(frames_total, -1)]
    unnamed x5 -> x3, local copies, waits for them, and re-layouts: 8.44 us -> 2.39 us
    div x5 -> x0, other arithmetic: 5.05 us -> none  [the longest x4 5.04 us: filter_block(): factor = jnp.linalg.cholesky(inner_gram)]
  transfers between devices with their start and end apart: 1 -> 1, of which waited for: 0 -> 0; matrix products, arithmetic and copies ran while one was open for 1% -> 1% of each run, Pallas kernels for 0% -> 11%
where the time goes in v1:
time: 77.3 us; the launch traced here: 76.9 us
  Pallas kernels  56.3 us (73%)
  blocking collectives  15.4 us (20%)
  local copies, waits for them, and re-layouts  2.39 us (3%)
  starting transfers between devices  1.29 us (2%)
  other arithmetic  0.83 us (1%)
    pallas_call x1, Pallas kernels, find_bases(): pl.pallas_call(basis_kernel, out_shape=(jax.ShapeDtypeStruct((hold, tall,...  43.3 us
    all_to_all x1, blocking collectives, shards(): sums = lax.all_to_all(sums, axes, 0, 0, tiled=True)  15.4 us
    pallas_call x1, Pallas kernels, compound(): pl.pallas_call(functools.partial(region_kernel, order=order), grid=(hold,...  8.73 us
    pallas_call x1, Pallas kernels, close_border(): pl.pallas_call(border_kernel, grid=(1,), out_shape=(jax.ShapeDtypeStruct(...  2.88 us
    unnamed x3, local copies, waits for them, and re-layouts  2.39 us
  transfers between devices with their start and end apart: 1, of which 0 were waited for; matrix products, arithmetic and copies ran while one was open for 1% of the time, Pallas kernels for 11%

profile of v1, /device:TPU:0, one launch (start us, length us, event | category | flops | bytes accessed | tf_op | source)
XLA Modules:
  0.0 76.9 jit_solution(3998448858993164376)
XLA Ops:
  0.6 1.7 %copy.9.start_ref = f32[300,96]{1,0:T(8,128)} copy(f32[300,96]{0,1:T(8,128)} %param.9) | data formatting | bytes 230400 | tf_op args[4]
  2.3 43.3 %find_bases.1 = (bf16[5,304,128]{2,1,0:T(8,128)(2,1)}, bf16[96,1408]{1,0:T(8,128)(2,1)}) custom-call(s32[160]{0:T(256)} %frame_ref.3, s32[160]{0:T(256)} %clutter_ref.3, s32[160]{0:T(256)} %noise_ref.3, f32[300,96]{1,0:T(8,128)} %copy.9.start_ref, bf16[5,300,2048]{2,1,0:T(8,128)(2,1)} %lower_ref.1), custom_call_target="tpu_custom_call" | custom-call | tf_op jit(solution)/shard_map/find_bases/pallas_call | solution.py:182
  45.6 1.3 %collective-permute-start = (bf16[96,1408]{1,0:T(8,128)(2,1)}, bf16[96,1408]{1,0:T(8,128)(2,1)S(1)}, u32[]{:S(2)}, u32[]{:S(2)}) collective-permute-start(bf16[96,1408]{1,0:T(8,128)(2,1)} %get-tuple-element.9), channel_id=1, source_target_pairs={{1,0},{2,1},{3,2},{4,3},{5,4},{6,5},{7,6},{8,7},{9,8},{10,9},{11,1... | collective-permute-start | bytes 811016 | tf_op jit(solution)/shard_map/ppermute | solution.py:355
  46.9 0.8 %sine_multiply_fusion.window_ref = f32[1,2048]{1,0:T(1,128)} fusion(), kind=kLoop, calls=%fused_computation | loop fusion | flops 6144 | bytes 8192 | tf_op jit(solution)/shard_map/integer_pow | solution.py:352
  47.7 8.7 %compound.1 = (f32[300,5120]{1,0:T(8,128)}, f32[1,5120]{1,0:T(1,128)}) custom-call(s32[160]{0:T(256)} %frame_ref.3, s32[160]{0:T(256)} %clutter_ref.3, s32[160]{0:T(256)} %noise_ref.3, f32[1,2048]{1,0:T(1,128)} %sine_multiply_fusion.window_ref, bf16[5,300,2048]{2,1,0:T(8,128)(2,1)} %lower_ref.1, bf16[5,300,2048]{2,1,0:T(8,128)(2,1)} %lower_ref.1, ...), custom_call_target="tpu_custom_call" | custom-call | flops 1179648000 | bytes 12288000 | tf_op jit(solution)/shard_map/compound/pallas_call | solution.py:258
  56.5 0.0 collective-permute-done.border_ref
  56.5 0.0 copy-start
  56.5 0.7 copy-done
  57.2 2.9 %close_border.1 = (f32[300,5120]{1,0:T(8,128)}, f32[1,5120]{1,0:T(1,128)}, f32[32,128]{1,0:T(8,128)}) custom-call(f32[1,2048]{1,0:T(1,128)} %sine_multiply_fusion.window_ref, bf16[96,1408]{1,0:T(8,128)(2,1)} %copy-done, f32[300,5120]{1,0:T(8,128)} %get-tuple-element.11.region_ref, ...), custom_call_target="tpu_custom_call", output_to_operand_aliasing={{0}: (2, {})} | custom-call | tf_op jit(solution)/shard_map/close_border/pallas_call | solution.py:306
  60.1 15.4 %all_to_all.11 = f32[32,1,128]{2,1,0:T(1,128)} all-to-all(f32[32,1,128]{2,1,0:T(1,128)} %bitcast.5), channel_id=1, replica_groups=mesh['space'=16,'grp'=2] {'space','grp'}, dimensions={0} | all-to-all | bytes 32768 | tf_op jit(solution)/shard_map/all_to_all | solution.py:360
  75.4 1.5 %relative_power.1 = f32[5120]{0:T(1024)} custom-call(f32[1,5120]{1,0:T(1,128)} %get-tuple-element.14.strength_ref, f32[32,128]{1,0:T(8,128)} %bitcast.4), custom_call_target="tpu_custom_call" | custom-call | tf_op jit(solution)/shard_map/relative_power/pallas_call | solution.py:338
Async XLA Ops:
  45.6 10.9 %collective-permute-start = (bf16[96,1408]{1,0:T(8,128)(2,1)}, bf16[96,1408]{1,0:T(8,128)(2,1)S(1)}, u32[]{:S(2)}, u32[]{:S(2)}) collective-permute-start(bf16[96,1408]{1,0:T(8,128)(2,1)} %get-tuple-element.9), channel_id=1, source_target_pairs={{1,0},{2,1},{3,2},{4,3},{5,4},{6,5},{7,6},{8,7},{9,8},{10,9},{11,1... | collective-permute-start | bytes 811016 | tf_op jit(solution)/shard_map/ppermute | solution.py:355
  56.5 0.7 copy-start

commit v2 on v1

v2 whole, which is shorter than its diff:
```python
import jax
import jax.numpy as jnp
import numpy as np
from jax import lax
from jax.experimental import pallas as pl
from jax.experimental.pallas import tpu as pltpu
from jax.sharding import PartitionSpec as P

ITERS = 4
LANES = 128
SLOTS = 8
PANEL = 12
SUPER = 24
CHUNK = 512
SIDE = 256
VMEM_LIMIT = 24 << 20
WIDE_LIMIT = 58 << 20


def round_up(value, unit):
    return -(-value // unit) * unit


def device_index():
    return lax.axis_index("space") * lax.axis_size("grp") + lax.axis_index("grp")


def two_parts(value):
    high = value.astype(jnp.bfloat16)
    return high, (value - high.astype(jnp.float32)).astype(jnp.bfloat16)


def three_parts(value):
    high = value.astype(jnp.bfloat16)
    rest = value - high.astype(jnp.float32)
    middle = rest.astype(jnp.bfloat16)
    return high, middle, (rest - middle.astype(jnp.float32)).astype(jnp.bfloat16)


def matmul(left, right, left_axis=1, right_axis=0):
    return lax.dot_general(
        left,
        right,
        (((left_axis,), (right_axis,)), ((), ())),
        preferred_element_type=jnp.float32,
    )


def inverse_factors(rows_ref, scaled_ref, out_ref, order, hold, out_stride):
    lane = lax.broadcasted_iota(jnp.int32, (SLOTS, LANES), 1)

    def spread(value, index):
        return jnp.broadcast_to(value[:, index : index + 1], (SLOTS, LANES))

    for start in range(0, order, SUPER):
        stop = min(start + SUPER, order)
        for base in range(start, stop, PANEL):
            panel = (lane >= base) & (lane < base + PANEL)
            rows = [rows_ref[(base + r) * SLOTS : (base + r + 1) * SLOTS, :] for r in range(PANEL)]
            block = {
                (r, c): spread(rows[r], base + c) for c in range(PANEL) for r in range(c + 1)
            }
            rows = [
                jnp.where(panel, jnp.where(lane == base + r, 1.0, 0.0), rows[r])
                for r in range(PANEL)
            ]
            scaled = []
            for j in range(PANEL):
                inverse = 1.0 / block[j, j]
                scaled.append(rows[j] * inverse)
                for r in range(j + 1, PANEL):
                    factor = block[j, r] * inverse
                    rows[r] = rows[r] - factor * rows[j]
                    for c in range(r, PANEL):
                        block[r, c] = block[r, c] - factor * block[j, c]
            for j in range(PANEL):
                out_ref[pl.ds(base + j, SLOTS, stride=out_stride), :] = jnp.where(
                    lane < base + PANEL, rows[j] * lax.rsqrt(block[j, j]), 0.0
                )
            if stop < order:
                later = (lane >= base + PANEL) & (lane < stop)
                for j in range(PANEL):
                    rows_ref[(base + j) * SLOTS : (base + j + 1) * SLOTS, :] = jnp.where(
                        later, 0.0, rows[j]
                    )
                    at = base - start + j
                    scaled_ref[at * SLOTS : (at + 1) * SLOTS, :] = scaled[j]
            for r in range(base + PANEL, stop):
                total = jnp.where(panel, 0.0, rows_ref[r * SLOTS : (r + 1) * SLOTS, :])
                for j in range(PANEL):
                    total = total - spread(scaled[j], r) * rows[j]
                rows_ref[r * SLOTS : (r + 1) * SLOTS, :] = total
        if stop < order:
            rest = order - stop
            wide_lane = lax.broadcasted_iota(jnp.int32, (rest, LANES), 1)
            done = (wide_lane >= start) & (wide_lane < stop)
            for b in range(hold):
                upper = rows_ref[pl.ds(start * SLOTS + b, stop - start, stride=SLOTS), :]
                lower = scaled_ref[pl.ds(b, stop - start, stride=SLOTS), :]
                u1, u2, u3 = three_parts(upper)
                l1, l2, l3 = three_parts(lower)
                update = matmul(
                    jnp.concatenate([l1, l1, l1, l2, l2, l3], axis=0),
                    jnp.concatenate([u1, u2, u3, u1, u2, u1], axis=0),
                    0,
                    0,
                )[stop:order, :]
                where = pl.ds(stop * SLOTS + b, rest, stride=SLOTS)
                rows_ref[where, :] = jnp.where(done, 0.0, rows_ref[where, :]) - update


def basis_kernel(
    frame_hbm,
    clutter_hbm,
    noise_hbm,
    start_hbm,
    window_hbm,
    echo_hbm,
    basis_ref,
    kept_ref,
    border_ref,
    frame_ref,
    clutter_ref,
    noise_ref,
    start_ref,
    window_ref,
    small_sems,
    echo_ref,
    sems,
    gram_ref,
    sub_ref,
    prod_ref,
    rows_ref,
    scaled_ref,
    factor_ref,
):
    hold, frames, width = echo_hbm.shape
    order = start_ref.shape[0]
    tall = basis_ref.shape[1]
    deep = sub_ref.shape[1]
    half = width // 2
    first = device_index() * hold
    pairs = (
        (start_hbm, start_ref),
        (frame_hbm, frame_ref),
        (clutter_hbm, clutter_ref),
        (noise_hbm, noise_ref),
        (window_hbm, window_ref),
    )
    small = [
        pltpu.make_async_copy(source, target, small_sems.at[number])
        for number, (source, target) in enumerate(pairs)
    ]
    copies = [
        pltpu.make_async_copy(echo_hbm.at[b], echo_ref.at[b], sems.at[b]) for b in range(hold)
    ]
    for copy in (copies[0], *small, *copies[1:]):
        copy.start()
    sub_ref[...] = jnp.zeros_like(sub_ref)
    prod_ref[...] = jnp.zeros_like(prod_ref)
    rows_ref[...] = jnp.zeros_like(rows_ref)
    factor_ref[...] = jnp.zeros_like(factor_ref)
    gram_ref[...] = jnp.zeros_like(gram_ref)
    for copy in small:
        copy.wait()
    high, low = two_parts(start_ref[...].T)
    for b in range(hold):
        sub_ref[b, :frames, :order] = high
        sub_ref[b, :frames, LANES : LANES + order] = low
    row_at = lax.broadcasted_iota(jnp.int32, (frames, frames), 0)
    column_at = lax.broadcasted_iota(jnp.int32, (frames, frames), 1)
    for b in range(hold):
        copies[b].wait()
        echo = echo_ref[b]
        valid = frame_ref[first + b]
        gram = matmul(echo, echo, 1, 1)
        padding = jnp.where((row_at == column_at) & (row_at >= valid), 1.0, 0.0)
        gram = jnp.where((row_at < valid) & (column_at < valid), gram, padding)
        high, low = two_parts(gram)
        gram_ref[b, :frames, :frames] = high
        gram_ref[b, tall : tall + frames, :frames] = low

    def iteration(_, carry):
        for b in range(hold):
            terms = matmul(gram_ref[b], sub_ref[b])
            terms = terms[:tall, :] + terms[tall:, :]
            high, low = two_parts(terms[:, :LANES] + terms[:, LANES:])
            prod_ref[b, :tall, :LANES] = high
            prod_ref[b, :tall, LANES:] = low
        for b in range(hold):
            whole = prod_ref[b]
            terms = matmul(whole, whole, 0, 0)
            terms = terms[:order, :] + terms[LANES : LANES + order, :]
            rows_ref[pl.ds(b, order, stride=SLOTS), :] = terms[:, :LANES] + terms[:, LANES:]
        inverse_factors(rows_ref, scaled_ref, factor_ref, order, hold, LANES)
        for b in range(hold):
            high, low = two_parts(factor_ref[b * LANES : (b + 1) * LANES, :])
            right = jnp.concatenate(
                [
                    jnp.concatenate([high, high], axis=1),
                    jnp.concatenate([low, low], axis=1),
                ],
                axis=0,
            )
            terms = matmul(prod_ref[b, :tall, :], right, 1, 1)
            high, low = two_parts(terms[:, :LANES] + terms[:, LANES:])
            sub_ref[b, :tall, :LANES] = high
            sub_ref[b, :tall, LANES:] = low
        return carry

    lax.fori_loop(0, ITERS, iteration, 0)
    frame_at = lax.broadcasted_iota(jnp.int32, (order, deep), 1)
    column_at = lax.broadcasted_iota(jnp.int32, (order, deep), 0)
    for b in range(hold):
        basis_ref[b] = sub_ref[b, :tall, :LANES]
        flipped = sub_ref[b, :, :LANES].T[:order, :]
        at = first + b
        band = (column_at >= clutter_ref[at]) & (column_at < noise_ref[at])
        kept_ref[b] = jnp.where(
            band & (frame_at < frame_ref[at]), flipped, jnp.zeros((), jnp.bfloat16)
        )
    pieces = half // SIDE
    for piece in range(pieces):
        at = slice(piece * SIDE, (piece + 1) * SIDE)
        part = matmul(kept_ref[0, :, :frames], echo_ref[0, :, at]) * window_ref[:, at]
        border_ref[piece * order : (piece + 1) * order, :] = part.astype(jnp.bfloat16)
    start = pieces * order
    high_rows = border_ref.shape[0] - start
    border_ref[start:, :LANES] = sub_ref[0, :high_rows, :LANES]
    border_ref[start:, LANES:] = sub_ref[0, high_rows : 2 * high_rows, :LANES]


def find_bases(echoes, window, frame_count, clutter_rank, noise_rank, start_basis):
    hold, frames, width = echoes.shape
    order = start_basis.shape[1]
    tall = round_up(frames, 16)
    deep = round_up(frames, LANES)
    outside = pl.BlockSpec(memory_space=pltpu.HBM)
    vmem = pl.BlockSpec(memory_space=pltpu.VMEM)
    return pl.pallas_call(
        basis_kernel,
        out_shape=(
            jax.ShapeDtypeStruct((hold, tall, LANES), jnp.bfloat16),
            jax.ShapeDtypeStruct((hold, order, deep), jnp.bfloat16),
            jax.ShapeDtypeStruct(
                (width // 2 // SIDE * order + round_up(tall // 2, 16), SIDE), jnp.bfloat16
            ),
        ),
        in_specs=[outside] * 6,
        out_specs=(vmem, vmem, vmem),
        scratch_shapes=[
            pltpu.SMEM(frame_count.shape, jnp.int32),
            pltpu.SMEM(clutter_rank.shape, jnp.int32),
            pltpu.SMEM(noise_rank.shape, jnp.int32),
            pltpu.VMEM((order, frames), jnp.float32),
            pltpu.VMEM(window.shape, jnp.float32),
            pltpu.SemaphoreType.DMA((5,)),
            pltpu.VMEM((hold, frames, width), jnp.bfloat16),
            pltpu.SemaphoreType.DMA((hold,)),
            pltpu.VMEM((hold, 2 * tall, deep), jnp.bfloat16),
            pltpu.VMEM((hold, deep, 2 * LANES), jnp.bfloat16),
            pltpu.VMEM((hold, deep, 2 * LANES), jnp.bfloat16),
            pltpu.VMEM((order * SLOTS, LANES), jnp.float32),
            pltpu.VMEM((SUPER * SLOTS, LANES), jnp.float32),
            pltpu.VMEM((SLOTS * LANES, LANES), jnp.float32),
        ],
        name="find_bases",
    )(frame_count, clutter_rank, noise_rank, start_basis.T, window, echoes)


def region_kernel(
    window_ref,
    kept_ref,
    basis_ref,
    echo_hbm,
    volume_hbm,
    strength_ref,
    last_ref,
    echo_ref,
    coef_ref,
    volume_ref,
    load_sems,
    store_sems,
):
    hold, frames, width = echo_hbm.shape
    order = kept_ref.shape[1]
    half = width // 2
    pieces = half // CHUNK
    sides = ((1, 0), (0, 1))
    loads = {}
    for region in range(hold):
        for side, shift in sides:
            block = region + shift
            if block < hold:
                at = slice(side * half, (side + 1) * half)
                loads[region, side] = pltpu.make_async_copy(
                    echo_hbm.at[block, :, at],
                    echo_ref.at[block, :, at],
                    load_sems.at[2 * region + side],
                )
    for load in loads.values():
        load.start()
    coef_ref[...] = jnp.zeros_like(coef_ref)
    stores = []
    for step in range(hold + 1):
        for side, shift in sides:
            block = step + shift
            if step == hold or block == hold:
                continue
            loads[step, side].wait()
            for left in range(0, half, CHUNK):
                at = slice(left, left + CHUNK)
                whole = slice(side * half + left, side * half + left + CHUNK)
                part = matmul(kept_ref[block, :, :frames], echo_ref[block, :, whole])
                part = (part * window_ref[:, whole]).astype(jnp.bfloat16)
                if step == hold - 1:
                    last_ref[:, at] = part
                else:
                    top = (1 - side) * LANES
                    coef_ref[step, top : top + order, at] = part
        region = step - 1
        if region < 0 or region == hold - 1:
            continue
        pair = jnp.concatenate([basis_ref[region, :frames], basis_ref[region + 1, :frames]], axis=1)
        for piece in range(pieces):
            at = slice(piece * CHUNK, (piece + 1) * CHUNK)
            both = matmul(pair, coef_ref[region, :, at])
            where = slice(region * half + piece * CHUNK, region * half + (piece + 1) * CHUNK)
            volume_ref[:, where] = both
            strength_ref[:, where] = jnp.sum(both * both, axis=0, keepdims=True) / frames
            store = pltpu.make_async_copy(
                volume_ref.at[:, where],
                volume_hbm.at[:, where],
                store_sems.at[region * pieces + piece],
            )
            store.start()
            stores.append(store)
    for store in stores:
        store.wait()


def compound(echoes, kept, basis, window):
    hold, frames, width = echoes.shape
    order = kept.shape[1]
    half = width // 2
    inside = (hold - 1) * half
    vmem = pl.BlockSpec(memory_space=pltpu.VMEM)
    outside = pl.BlockSpec(memory_space=pltpu.HBM)
    return pl.pallas_call(
        region_kernel,
        out_shape=(
            jax.ShapeDtypeStruct((frames, hold * half), jnp.float32),
            jax.ShapeDtypeStruct((1, inside), jnp.float32),
            jax.ShapeDtypeStruct((order, half), jnp.bfloat16),
        ),
        in_specs=[vmem, vmem, vmem, outside],
        out_specs=(outside, vmem, vmem),
        scratch_shapes=[
            pltpu.VMEM((hold, frames, width), jnp.bfloat16),
            pltpu.VMEM((hold - 1, 2 * LANES, half), jnp.bfloat16),
            pltpu.VMEM((frames, inside), jnp.float32),
            pltpu.SemaphoreType.DMA((2 * hold,)),
            pltpu.SemaphoreType.DMA((inside // CHUNK,)),
        ],
        cost_estimate=pl.CostEstimate(
            flops=hold * 4 * frames * order * width,
            bytes_accessed=hold * frames * width * 4,
            transcendentals=0,
        ),
        compiler_params=pltpu.CompilerParams(vmem_limit_bytes=WIDE_LIMIT),
        name="compound",
    )(window, kept, basis, echoes)


def border_kernel(
    strength_hbm,
    own_hbm,
    basis_hbm,
    border_hbm,
    volume_in,
    volume_hbm,
    all_hbm,
    sums_ref,
    strength_ref,
    coef_ref,
    basis_ref,
    border_ref,
    volume_ref,
    load_sems,
    store_sems,
):
    frames, half = volume_ref.shape
    order = own_hbm.shape[0]
    hold = basis_hbm.shape[0]
    inside = strength_hbm.shape[1]
    pairs = (
        (border_hbm, border_ref),
        (own_hbm, coef_ref.at[:order]),
        (basis_hbm.at[hold - 1], basis_ref),
        (strength_hbm, strength_ref.at[:, :inside]),
    )
    loads = [
        pltpu.make_async_copy(source, target, load_sems.at[number])
        for number, (source, target) in enumerate(pairs)
    ]
    for load in loads:
        load.start()
    for top in (order, LANES + order):
        coef_ref[top : top + LANES - order, :] = jnp.zeros((LANES - order, half), jnp.bfloat16)
    for load in loads:
        load.wait()
    total = jnp.sum(strength_ref[:, :inside], axis=1, keepdims=True)
    start = half // SIDE * order
    following = jnp.concatenate([border_ref[start:, :LANES], border_ref[start:, LANES:]], axis=0)
    pair = jnp.concatenate([basis_ref[:frames], following[:frames]], axis=1)
    stores = []
    for number, left in enumerate(range(0, half, SIDE)):
        at = slice(left, left + SIDE)
        where = slice(inside + left, inside + left + SIDE)
        coef_ref[LANES : LANES + order, at] = border_ref[number * order : (number + 1) * order, :]
        both = matmul(pair, coef_ref[:, at])
        volume_ref[:, at] = both
        last = jnp.sum(both * both, axis=0, keepdims=True) / frames
        strength_ref[:, where] = last
        total = total + jnp.sum(last, axis=1, keepdims=True)
        store = pltpu.make_async_copy(
            volume_ref.at[:, at], volume_hbm.at[:, where], store_sems.at[number]
        )
        store.start()
        stores.append(store)
    store = pltpu.make_async_copy(strength_ref, all_hbm, store_sems.at[len(stores)])
    store.start()
    stores.append(store)
    sums_ref[...] = jnp.broadcast_to(total, sums_ref.shape)
    for store in stores:
        store.wait()


def close_border(own, basis, border, volume, strength, devices):
    order, half = own.shape
    frames, voxels = volume.shape
    tall = basis.shape[1]
    outside = pl.BlockSpec(memory_space=pltpu.HBM)
    anywhere = pl.BlockSpec(memory_space=pl.ANY)
    return pl.pallas_call(
        border_kernel,
        out_shape=(
            jax.ShapeDtypeStruct(volume.shape, jnp.float32),
            jax.ShapeDtypeStruct((1, voxels), jnp.float32),
            jax.ShapeDtypeStruct((devices, LANES), jnp.float32),
        ),
        in_specs=[anywhere] * 4 + [outside],
        out_specs=(outside, anywhere, pl.BlockSpec(memory_space=pltpu.VMEM)),
        scratch_shapes=[
            pltpu.VMEM((1, voxels), jnp.float32),
            pltpu.VMEM((2 * LANES, half), jnp.bfloat16),
            pltpu.VMEM((tall, LANES), jnp.bfloat16),
            pltpu.VMEM(border.shape, jnp.bfloat16),
            pltpu.VMEM((frames, half), jnp.float32),
            pltpu.SemaphoreType.DMA((4,)),
            pltpu.SemaphoreType.DMA((1 + half // SIDE,)),
        ],
        input_output_aliases={4: 0},
        compiler_params=pltpu.CompilerParams(vmem_limit_bytes=VMEM_LIMIT),
        name="close_border",
    )(strength, own, basis, border, volume)


def power_kernel(strength_ref, sums_ref, power_ref):
    voxels = strength_ref.shape[1] * sums_ref.shape[0]
    total = jnp.sum(sums_ref[:, :1])
    power_ref[...] = (strength_ref[...] / (total / voxels + 1e-06))[0]


def relative_power(strength, sums):
    vmem = pl.BlockSpec(memory_space=pltpu.VMEM)
    return pl.pallas_call(
        power_kernel,
        out_shape=jax.ShapeDtypeStruct((strength.shape[1],), jnp.float32),
        in_specs=[vmem, vmem],
        out_specs=vmem,
        compiler_params=pltpu.CompilerParams(vmem_limit_bytes=VMEM_LIMIT),
        name="relative_power",
    )(strength, sums)


def shards(echoes, frame_count, clutter_rank, noise_rank, start_basis):
    axes = ("space", "grp")
    devices = lax.axis_size("space") * lax.axis_size("grp")
    hold, frames, width = echoes.shape
    window = np.sin(np.pi * (np.arange(width) + 0.5) / width) ** 2
    window = jnp.asarray(window, jnp.float32)[None, :]
    basis, kept, border = find_bases(
        echoes, window, frame_count, clutter_rank, noise_rank, start_basis
    )
    border = lax.ppermute(border, axes, [(source, source - 1) for source in range(1, devices)])
    volume, strength, own = compound(echoes, kept, basis, window)
    volume, strength, sums = close_border(own, basis, border, volume, strength, devices)
    sums = lax.all_to_all(sums, axes, 0, 0, tiled=True)
    return volume, relative_power(strength, sums)


def solution(mesh):
    return jax.shard_map(
        shards,
        mesh=mesh,
        in_specs=(P(("space", "grp"), None, None), P(), P(), P(), P()),
        out_specs=(P(None, ("space", "grp")), P(("space", "grp"))),
        check_vma=False,
    )
```

time: 77.3 us -> 57.8 us (0.75)
  Pallas kernels: 56.3 us -> 38.7 us
  other arithmetic: 0.83 us -> 0 us
    pallas_call x1, Pallas kernels: 43.3 us -> 28.8 us  [find_bases(): pl.pallas_call(basis_kernel, out_shape=(jax.ShapeDtypeStruct((hold, tall,...]
    pallas_call x2, Pallas kernels: 11.6 us -> 9.12 us  [the longest x1 7.35 us: compound(): pl.pallas_call(region_kernel, out_shape=(jax.ShapeDtypeStruct((frames, ho...]
    integer_pow x1 -> x0, other arithmetic: 0.83 us -> none  [shards(): jnp.sin(jnp.pi * (jnp.arange(width, dtype=jnp.float32) + 0.5) / width) ** 2]
    unnamed x3 -> x6, local copies, waits for them, and re-layouts: 2.39 us -> 1.64 us
  transfers between devices with their start and end apart: 1 -> 1, of which waited for: 0 -> 0; matrix products, arithmetic and copies ran while one was open for 1% -> 0% of each run, Pallas kernels for 11% -> 13%
where the time goes in v2:
time: 57.8 us; the launch traced here: 57.5 us
  Pallas kernels  38.7 us (67%)
  blocking collectives  15 us (26%)
  local copies, waits for them, and re-layouts  1.64 us (3%)
  starting transfers between devices  1.42 us (2%)
  between operations  0.7 us (1%)
    pallas_call x1, Pallas kernels, find_bases(): pl.pallas_call(basis_kernel, out_shape=(jax.ShapeDtypeStruct((hold, tall,...  28.8 us
    all_to_all x1, blocking collectives, shards(): sums = lax.all_to_all(sums, axes, 0, 0, tiled=True)  15 us
    pallas_call x1, Pallas kernels, compound(): pl.pallas_call(region_kernel, out_shape=(jax.ShapeDtypeStruct((frames, ho...  7.35 us
    pallas_call x1, Pallas kernels, close_border(): pl.pallas_call(border_kernel, out_shape=(jax.ShapeDtypeStruct(volume.shap...  1.78 us
    unnamed x6, local copies, waits for them, and re-layouts  1.64 us
    ppermute x1, starting transfers between devices, shards(): lax.ppermute(border, axes, [(source, source - 1) for source in range(1, d...  1.42 us
  transfers between devices with their start and end apart: 1, of which 0 were waited for; matrix products, arithmetic and copies ran while one was open for 0% of the time, Pallas kernels for 13%

profile of v2, /device:TPU:0, one launch (start us, length us, event | category | flops | bytes accessed | tf_op | source)
XLA Modules:
  0.0 57.5 jit_solution(18183622859861788665)
XLA Ops:
  0.6 28.8 %find_bases.1 = (bf16[5,304,128]{2,1,0:T(8,128)(2,1)}, bf16[5,96,384]{2,1,0:T(8,128)(2,1)}, bf16[544,256]{1,0:T(8,128)(2,1)}) custom-call(s32[160]{0:T(256)} %frame_hbm.1, s32[160]{0:T(256)} %clutter_hbm.1, s32[160]{0:T(256)} %noise_hbm.1, f32[96,300]{1,0:T(8,128)} %bitcast.7, f32[1,2048]{1,0:T(1,128)} %constant.4.window_hbm.window_ref, ...), custom_call_target="tpu_custom_call" | custom-call | tf_op jit(solution)/shard_map/find_bases/pallas_call | solution.py:240
  29.5 0.0 copy-start
  29.5 1.4 %collective-permute-start = (bf16[544,256]{1,0:T(8,128)(2,1)}, bf16[544,256]{1,0:T(8,128)(2,1)S(1)}, u32[]{:S(2)}, u32[]{:S(2)}) collective-permute-start(bf16[544,256]{1,0:T(8,128)(2,1)} %get-tuple-element.15), channel_id=1, source_target_pairs={{1,0},{2,1},{3,2},{4,3},{5,4},{6,5},{7,6},{8,7},{9,8},{10,9},{11,1... | collective-permute-start | bytes 835592 | tf_op jit(solution)/shard_map/ppermute | solution.py:496
  30.9 7.3 %compound.1 = (f32[300,5120]{1,0:T(8,128)}, f32[1,4096]{1,0:T(1,128)}, bf16[96,1024]{1,0:T(8,128)(2,1)}) custom-call(f32[1,2048]{1,0:T(1,128)} %constant.4.window_hbm.window_ref, bf16[5,96,384]{2,1,0:T(8,128)(2,1)} %get-tuple-element.11.kept_ref, bf16[5,304,128]{2,1,0:T(8,128)(2,1)} %get-tuple-element.12.basis_ref.basis_hbm, bf16[5,300,2048]{2,1,0:T(8,128)(2,1)} %echo_hbm.3), custom_call_target="tpu_custom_call" | custom-call | flops 1179648000 | bytes 12288000 | tf_op jit(solution)/shard_map/compound/pallas_call | solution.py:349
  38.3 0.0 collective-permute-done.border_hbm
  38.3 0.0 copy-done
  38.3 0.0 copy-start.1
  38.3 0.9 %copy-done.1 = bf16[96,1024]{1,0:T(8,128)(2,1)S(1)} copy-done((bf16[96,1024]{1,0:T(8,128)(2,1)S(1)}, bf16[96,1024]{1,0:T(8,128)(2,1)}, u32[]{:S(2)}) %copy-start.1) | copy-done | bytes 196632
  39.2 0.0 copy-start.2
  39.2 0.7 %copy-done.2 = f32[1,4096]{1,0:T(1,128)S(1)} copy-done((f32[1,4096]{1,0:T(1,128)S(1)}, f32[1,4096]{1,0:T(1,128)}, u32[]{:S(2)}) %copy-start.2) | copy-done | bytes 16408
  39.9 1.8 %close_border.1 = (f32[300,5120]{1,0:T(8,128)}, f32[1,5120]{1,0:T(1,128)S(1)}, f32[32,128]{1,0:T(8,128)S(1)}) custom-call(f32[1,4096]{1,0:T(1,128)S(1)} %copy-done.2, bf16[96,1024]{1,0:T(8,128)(2,1)S(1)} %copy-done.1, bf16[5,304,128]{2,1,0:T(8,128)(2,1)S(1)} %copy-done, ...), custom_call_target="tpu_custom_call", output_to_operand_aliasing={{0}: (4, {})} | custom-call | tf_op jit(solution)/shard_map/close_border/pallas_call | solution.py:445
  41.7 15.0 %all_to_all.11 = f32[32,1,128]{2,1,0:T(1,128)S(1)} all-to-all(f32[32,1,128]{2,1,0:T(1,128)S(1)} %bitcast.6), channel_id=1, replica_groups=mesh['space'=16,'grp'=2] {'space','grp'}, dimensions={0} | all-to-all | bytes 32768 | tf_op jit(solution)/shard_map/all_to_all | solution.py:499
  56.7 0.7 %relative_power.1 = f32[5120]{0:T(1024)} custom-call(f32[1,5120]{1,0:T(1,128)S(1)} %get-tuple-element.18.strength_ref, f32[32,128]{1,0:T(8,128)S(1)} %bitcast.5), custom_call_target="tpu_custom_call" | custom-call | tf_op jit(solution)/shard_map/relative_power/pallas_call | solution.py:477
Async XLA Ops:
  29.5 8.8 %copy-start = (bf16[5,304,128]{2,1,0:T(8,128)(2,1)S(1)}, bf16[5,304,128]{2,1,0:T(8,128)(2,1)}, u32[]{:S(2)}) copy-start(bf16[5,304,128]{2,1,0:T(8,128)(2,1)} %get-tuple-element.12.basis_ref.basis_hbm) | copy-start | bytes 1167364
  29.5 8.8 %collective-permute-start = (bf16[544,256]{1,0:T(8,128)(2,1)}, bf16[544,256]{1,0:T(8,128)(2,1)S(1)}, u32[]{:S(2)}, u32[]{:S(2)}) collective-permute-start(bf16[544,256]{1,0:T(8,128)(2,1)} %get-tuple-element.15), channel_id=1, source_target_pairs={{1,0},{2,1},{3,2},{4,3},{5,4},{6,5},{7,6},{8,7},{9,8},{10,9},{11,1... | collective-permute-start | bytes 835592 | tf_op jit(solution)/shard_map/ppermute | solution.py:496
  38.3 0.9 %copy-start.1 = (bf16[96,1024]{1,0:T(8,128)(2,1)S(1)}, bf16[96,1024]{1,0:T(8,128)(2,1)}, u32[]{:S(2)}) copy-start(bf16[96,1024]{1,0:T(8,128)(2,1)} %get-tuple-element.14.own_hbm) | copy-start | bytes 589828
  39.2 0.7 %copy-start.2 = (f32[1,4096]{1,0:T(1,128)S(1)}, f32[1,4096]{1,0:T(1,128)}, u32[]{:S(2)}) copy-start(f32[1,4096]{1,0:T(1,128)} %get-tuple-element.13.strength_hbm) | copy-start | bytes 49156

commit v3 on v2

--- a/solution.py
+++ b/solution.py
@@ -14,7 +14,7 @@
 CHUNK = 512
 SIDE = 256
 VMEM_LIMIT = 24 << 20
-WIDE_LIMIT = 58 << 20
+WIDE_LIMIT = 50 << 20
 
 
 def round_up(value, unit):

time: 57.8 us -> 56.7 us (0.981)
  Pallas kernels: 38.7 us -> 37.4 us
    pallas_call x1, Pallas kernels: 7.35 us -> 5.54 us  [compound(): pl.pallas_call(region_kernel, out_shape=(jax.ShapeDtypeStruct((frames, ho...]
  transfers between devices with their start and end apart: 1 -> 1, of which waited for: 0 -> 0; matrix products, arithmetic and copies ran while one was open for 0% -> 0% of each run, Pallas kernels for 13% -> 10%
where the time goes in v3:
time: 56.7 us; the launch traced here: 56.4 us
  Pallas kernels  37.4 us (66%)
  blocking collectives  15.1 us (27%)
  local copies, waits for them, and re-layouts  1.98 us (3%)
  starting transfers between devices  1.29 us (2%)
  between operations  0.7 us (1%)
    pallas_call x1, Pallas kernels, find_bases(): pl.pallas_call(basis_kernel, out_shape=(jax.ShapeDtypeStruct((hold, tall,...  29.3 us
    all_to_all x1, blocking collectives, shards(): sums = lax.all_to_all(sums, axes, 0, 0, tiled=True)  15.1 us
    pallas_call x1, Pallas kernels, compound(): pl.pallas_call(region_kernel, out_shape=(jax.ShapeDtypeStruct((frames, ho...  5.54 us
    unnamed x6, local copies, waits for them, and re-layouts  1.98 us
    pallas_call x1, Pallas kernels, close_border(): pl.pallas_call(border_kernel, out_shape=(jax.ShapeDtypeStruct(volume.shap...  1.79 us
    ppermute x1, starting transfers between devices, shards(): lax.ppermute(border, axes, [(source, source - 1) for source in range(1, d...  1.29 us
  transfers between devices with their start and end apart: 1, of which 0 were waited for; matrix products, arithmetic and copies ran while one was open for 0% of the time, Pallas kernels for 10%

profile of v3, /device:TPU:0, one launch (start us, length us, event | category | flops | bytes accessed | tf_op | source)
XLA Modules:
  0.0 56.4 jit_solution(14884569210466393608)
XLA Ops:
  0.6 0.0 copy-start.2
  0.6 29.3 %find_bases.1 = (bf16[5,304,128]{2,1,0:T(8,128)(2,1)}, bf16[5,96,384]{2,1,0:T(8,128)(2,1)}, bf16[544,256]{1,0:T(8,128)(2,1)}) custom-call(s32[160]{0:T(256)} %frame_hbm.1, s32[160]{0:T(256)} %clutter_hbm.1, s32[160]{0:T(256)} %noise_hbm.1, f32[96,300]{1,0:T(8,128)} %bitcast.7, f32[1,2048]{1,0:T(1,128)} %constant.4.window_hbm.window_ref, ...), custom_call_target="tpu_custom_call" | custom-call | tf_op jit(solution)/shard_map/find_bases/pallas_call | solution.py:240
  30.0 1.3 %collective-permute-start = (bf16[544,256]{1,0:T(8,128)(2,1)}, bf16[544,256]{1,0:T(8,128)(2,1)S(1)}, u32[]{:S(2)}, u32[]{:S(2)}) collective-permute-start(bf16[544,256]{1,0:T(8,128)(2,1)} %get-tuple-element.15), channel_id=1, source_target_pairs={{1,0},{2,1},{3,2},{4,3},{5,4},{6,5},{7,6},{8,7},{9,8},{10,9},{11,1... | collective-permute-start | bytes 835592 | tf_op jit(solution)/shard_map/ppermute | solution.py:496
  31.3 0.0 copy-done.2
  31.3 0.0 copy-start
  31.3 1.0 %copy-done = bf16[5,304,128]{2,1,0:T(8,128)(2,1)S(1)} copy-done((bf16[5,304,128]{2,1,0:T(8,128)(2,1)S(1)}, bf16[5,304,128]{2,1,0:T(8,128)(2,1)}, u32[]{:S(2)}) %copy-start) | copy-done | bytes 389144
  32.3 0.0 copy-start.1
  32.3 1.0 %copy-done.1 = bf16[5,96,384]{2,1,0:T(8,128)(2,1)S(1)} copy-done((bf16[5,96,384]{2,1,0:T(8,128)(2,1)S(1)}, bf16[5,96,384]{2,1,0:T(8,128)(2,1)}, u32[]{:S(2)}) %copy-start.1) | copy-done | bytes 368664
  33.3 5.5 %compound.1 = (f32[300,5120]{1,0:T(8,128)}, f32[1,4096]{1,0:T(1,128)S(1)}, bf16[96,1024]{1,0:T(8,128)(2,1)S(1)}) custom-call(f32[1,2048]{1,0:T(1,128)S(1)} %copy-done.2, bf16[5,96,384]{2,1,0:T(8,128)(2,1)S(1)} %copy-done.1, bf16[5,304,128]{2,1,0:T(8,128)(2,1)S(1)} %copy-done, bf16[5,300,2048]{2,1,0:T(8,128)(2,1)} %echo_hbm.3), custom_call_target="tpu_custom_call" | custom-call | flops 1179648000 | bytes 12288000 | tf_op jit(solution)/shard_map/compound/pallas_call | solution.py:349
  38.8 0.0 collective-permute-done.border_hbm
  38.8 1.8 %close_border.1 = (f32[300,5120]{1,0:T(8,128)}, f32[1,5120]{1,0:T(1,128)S(1)}, f32[32,128]{1,0:T(8,128)S(1)}) custom-call(f32[1,4096]{1,0:T(1,128)S(1)} %get-tuple-element.13.strength_hbm, bf16[96,1024]{1,0:T(8,128)(2,1)S(1)} %get-tuple-element.14.own_hbm, bf16[5,304,128]{2,1,0:T(8,128)(2,1)S(1)} %copy-done, ...), custom_call_target="tpu_custom_call", output_to_operand_aliasing={{0}: (4, {})} | custom-call | tf_op jit(solution)/shard_map/close_border/pallas_call | solution.py:445
  40.6 15.1 %all_to_all.11 = f32[32,1,128]{2,1,0:T(1,128)S(1)} all-to-all(f32[32,1,128]{2,1,0:T(1,128)S(1)} %bitcast.6), channel_id=1, replica_groups=mesh['space'=16,'grp'=2] {'space','grp'}, dimensions={0} | all-to-all | bytes 32768 | tf_op jit(solution)/shard_map/all_to_all | solution.py:499
  55.7 0.7 %relative_power.1 = f32[5120]{0:T(1024)} custom-call(f32[1,5120]{1,0:T(1,128)S(1)} %get-tuple-element.18.strength_ref, f32[32,128]{1,0:T(8,128)S(1)} %bitcast.5), custom_call_target="tpu_custom_call" | custom-call | tf_op jit(solution)/shard_map/relative_power/pallas_call | solution.py:477
Async XLA Ops:
  0.6 30.7 %copy-start.2 = (f32[1,2048]{1,0:T(1,128)S(1)}, f32[1,2048]{1,0:T(1,128)}, u32[]{:S(2)}) copy-start(f32[1,2048]{1,0:T(1,128)} %constant.4.window_hbm.window_ref) | copy-start | bytes 24580
  30.0 8.8 %collective-permute-start = (bf16[544,256]{1,0:T(8,128)(2,1)}, bf16[544,256]{1,0:T(8,128)(2,1)S(1)}, u32[]{:S(2)}, u32[]{:S(2)}) collective-permute-start(bf16[544,256]{1,0:T(8,128)(2,1)} %get-tuple-element.15), channel_id=1, source_target_pairs={{1,0},{2,1},{3,2},{4,3},{5,4},{6,5},{7,6},{8,7},{9,8},{10,9},{11,1... | collective-permute-start | bytes 835592 | tf_op jit(solution)/shard_map/ppermute | solution.py:496
  31.3 1.0 %copy-start = (bf16[5,304,128]{2,1,0:T(8,128)(2,1)S(1)}, bf16[5,304,128]{2,1,0:T(8,128)(2,1)}, u32[]{:S(2)}) copy-start(bf16[5,304,128]{2,1,0:T(8,128)(2,1)} %get-tuple-element.12.basis_ref.basis_hbm) | copy-start | bytes 1167364
  32.3 1.0 %copy-start.1 = (bf16[5,96,384]{2,1,0:T(8,128)(2,1)S(1)}, bf16[5,96,384]{2,1,0:T(8,128)(2,1)}, u32[]{:S(2)}) copy-start(bf16[5,96,384]{2,1,0:T(8,128)(2,1)} %get-tuple-element.11.kept_ref) | copy-start | bytes 1105924
